TPU v7x, 32 devices: a whole 2x2x4 slice. The times are simulated.
32 devices in a mesh: dp: 4 (over y, x), fsdp: 8 (over z, core).
Axes of the slice: x: 2, y: 2, z: 4, core: 2. Of those that a mesh axis runs over, the one named last changes fastest.
Arguments:
- tokens: bfloat16 [32, 1024, 768], P(('dp', 'fsdp')), may hold values from -6 to 6
- lengths: int32 [32], P(('dp', 'fsdp')), may hold values from 256 to 1024, as said below
- cells: int32 [32, 1024], P(('dp', 'fsdp')), may hold values 0 or 1
- cotangent: bfloat16 [32, 1024, 768], P(('dp', 'fsdp')), may hold values from -6 to 6
- ln1_gain: bfloat16 [768], P('fsdp'), may hold values from 0.5 to 1.5
- ln1_bias: bfloat16 [768], P('fsdp'), may hold values from -3 to 3
- w_qkv: bfloat16 [768, 2304], P('fsdp'), may hold values from -0.21875 to 0.21875
- b_query: bfloat16 [768], P('fsdp'), may hold values from -6 to 6
- b_value: bfloat16 [768], P('fsdp'), may hold values from -6 to 6
- w_out: bfloat16 [768, 768], P('fsdp'), may hold values from -0.875 to 0.875
- b_out: bfloat16 [768], P('fsdp'), may hold values from -3 to 3
- ln2_gain: bfloat16 [768], P('fsdp'), may hold values from 0.5 to 1.5
- ln2_bias: bfloat16 [768], P('fsdp'), may hold values from -3 to 3
- w_up: bfloat16 [768, 3072], P('fsdp'), may hold values from -0.21875 to 0.21875
- b_up: bfloat16 [3072], P('fsdp'), may hold values from -3 to 3
- w_down: bfloat16 [3072, 768], P('fsdp'), may hold values from -0.109375 to 0.109375
- b_down: bfloat16 [768], P('fsdp'), may hold values from -3 to 3
Outputs:
- output: bfloat16 [32, 1024, 768], P(('dp', 'fsdp'))
- grad_tokens: float32 [32, 1024, 768], P(('dp', 'fsdp'))
- grad_ln1_gain: float32 [768], P('fsdp')
- grad_ln1_bias: float32 [768], P('fsdp')
- grad_w_qkv: float32 [768, 2304], P('fsdp')
- grad_b_query: float32 [768], P('fsdp')
- grad_b_value: float32 [768], P('fsdp')
- grad_w_out: float32 [768, 768], P('fsdp')
- grad_b_out: float32 [768], P('fsdp')
- grad_ln2_gain: float32 [768], P('fsdp')
- grad_ln2_bias: float32 [768], P('fsdp')
- grad_w_up: float32 [768, 3072], P('fsdp')
- grad_b_up: float32 [3072], P('fsdp')
- grad_w_down: float32 [3072, 768], P('fsdp')
- grad_b_down: float32 [768], P('fsdp')
Inputs may be any that keep to these rules, and one draw needn't show every extreme that they name: `lengths`: each sequence has at least 256 valid tokens, and some sequence fills all 1024 slots.
All inputs are finite; a program needn't handle non-finite values. No bound on the sum of `cells` on one device may be relied on, other than what follows from the above.
Results may differ from a plain program's by a relative error of at most 0.019.
Values may be sent and summed in bfloat16 or wider, within the bound.
A program may use at most 128 MiB of HBM per device.

v0:
```python
from functools import partial
import math

import jax
import jax.numpy as jnp
from jax import lax
from jax.sharding import PartitionSpec as P

H = 12


EPSILON = 1e-05
GELU_C = 0.7978845608028654
GELU_A = 0.044715


def norm_forward(values):
    row_mean = jnp.mean(values, axis=-1, keepdims=True)
    centered = values - row_mean
    inv_std = lax.rsqrt(jnp.mean(centered * centered, axis=-1, keepdims=True) + EPSILON)
    return (centered * inv_std, inv_std)


def norm_backward(grad_normed, normalized, inv_std, gain):
    scaled = grad_normed * gain
    return inv_std * (
        scaled
        - jnp.mean(scaled, axis=-1, keepdims=True)
        - normalized * jnp.mean(scaled * normalized, axis=-1, keepdims=True)
    )


def gelu_pair(values):
    cubic = values * values * values
    tanh_part = jnp.tanh(GELU_C * (values + GELU_A * cubic))
    result = 0.5 * values * (1.0 + tanh_part)
    slope = 0.5 * (1.0 + tanh_part) + 0.5 * values * (1.0 - tanh_part * tanh_part) * GELU_C * (
        1.0 + 3.0 * GELU_A * values * values
    )
    return (result, slope)


def allowed_blocks(lengths, cells, context):
    positions = jnp.arange(context)
    query_pos = positions[None, :, None]
    key_pos = positions[None, None, :]
    usable = (key_pos <= query_pos) & (key_pos < lengths[:, None, None]) & (cells[:, None, :] == 1)
    return usable | (key_pos == query_pos)


def split_heads(rows, seqs, context, heads):
    width = rows.shape[1]
    return rows.reshape(seqs, context, heads, width // heads).transpose(2, 0, 1, 3)


def join_heads(stacked):
    return stacked.transpose(1, 2, 0, 3).reshape(-1, stacked.shape[0] * stacked.shape[3])


def head_forward(allowed, operands):
    query_head, key_head, value_head = operands
    scores = jnp.einsum("sqd,skd->sqk", query_head, key_head, preferred_element_type=jnp.float32)
    scores = jnp.where(allowed, scores, -1e30)
    row_max = jnp.max(scores, axis=-1, keepdims=True)
    exponent = jnp.exp(scores - row_max)
    row_total = jnp.sum(exponent, axis=-1, keepdims=True)
    softmax_rows = (exponent / row_total).astype(jnp.bfloat16)
    attended = jnp.einsum(
        "sqk,skd->sqd", softmax_rows, value_head, preferred_element_type=jnp.float32
    )
    return (attended, (row_max + jnp.log(row_total))[..., 0])


def head_backward(allowed, operands):
    query_head, key_head, value_head, grad_head, log_total = operands
    scores = jnp.einsum("sqd,skd->sqk", query_head, key_head, preferred_element_type=jnp.float32)
    softmax_rows = jnp.where(allowed, jnp.exp(scores - log_total[..., None]), 0.0)
    grad_values = jnp.einsum(
        "sqk,sqd->skd",
        softmax_rows.astype(jnp.bfloat16),
        grad_head,
        preferred_element_type=jnp.float32,
    )
    grad_probs = jnp.einsum(
        "sqd,skd->sqk", grad_head, value_head, preferred_element_type=jnp.float32
    )
    inner = jnp.sum(softmax_rows * grad_probs, axis=-1, keepdims=True)
    grad_scores = (softmax_rows * (grad_probs - inner)).astype(jnp.bfloat16)
    grad_queries = jnp.einsum(
        "sqk,skd->sqd", grad_scores, key_head, preferred_element_type=jnp.float32
    )
    grad_keys = jnp.einsum(
        "sqk,sqd->skd", grad_scores, query_head, preferred_element_type=jnp.float32
    )
    return (grad_queries, grad_keys, grad_values)


def per_device(
    tokens,
    lengths,
    cells,
    cotangent,
    ln1_gain,
    ln1_bias,
    w_qkv,
    b_query,
    b_value,
    w_out,
    b_out,
    ln2_gain,
    ln2_bias,
    w_up,
    b_up,
    w_down,
    b_down,
):
    seqs, context, width = tokens.shape
    heads = H
    scale = 1.0 / math.sqrt(width // heads)
    attn_parts = (
        lax.all_gather(ln1_gain, "fsdp", axis=0, tiled=True),
        lax.all_gather(ln1_bias, "fsdp", axis=0, tiled=True),
        lax.all_gather(w_qkv, "fsdp", axis=0, tiled=True),
        lax.all_gather(b_query, "fsdp", axis=0, tiled=True),
        lax.all_gather(b_value, "fsdp", axis=0, tiled=True),
        lax.all_gather(w_out, "fsdp", axis=0, tiled=True),
        lax.all_gather(b_out, "fsdp", axis=0, tiled=True),
    )
    gain_one, shift_one, qkv_full, bias_query, bias_value, out_full, bias_out = attn_parts
    inputs = tokens.reshape(-1, width).astype(jnp.float32)
    normal_one, inv_one = norm_forward(inputs)
    normed_one = (normal_one * gain_one.astype(jnp.float32) + shift_one.astype(jnp.float32)).astype(
        jnp.bfloat16
    )
    projected = jnp.dot(normed_one, qkv_full, preferred_element_type=jnp.float32)
    queries = ((projected[:, :width] + bias_query.astype(jnp.float32)) * scale).astype(jnp.bfloat16)
    key_rows = projected[:, width : 2 * width].astype(jnp.bfloat16)
    value_rows = (projected[:, 2 * width :] + bias_value.astype(jnp.float32)).astype(jnp.bfloat16)
    allowed = allowed_blocks(lengths, cells, context)
    query_heads = split_heads(queries, seqs, context, heads)
    key_heads = split_heads(key_rows, seqs, context, heads)
    value_heads = split_heads(value_rows, seqs, context, heads)
    attended_heads, log_totals = lax.map(
        partial(head_forward, allowed), (query_heads, key_heads, value_heads)
    )
    attended = join_heads(attended_heads).astype(jnp.bfloat16)
    middle = (
        inputs
        + jnp.dot(attended, out_full, preferred_element_type=jnp.float32)
        + bias_out.astype(jnp.float32)
    )
    mlp_parts = (
        lax.all_gather(ln2_gain, "fsdp", axis=0, tiled=True),
        lax.all_gather(ln2_bias, "fsdp", axis=0, tiled=True),
        lax.all_gather(w_up, "fsdp", axis=0, tiled=True),
        lax.all_gather(b_up, "fsdp", axis=0, tiled=True),
        lax.all_gather(w_down, "fsdp", axis=0, tiled=True),
        lax.all_gather(b_down, "fsdp", axis=0, tiled=True),
    )
    gain_two, shift_two, up_full, bias_up, down_full, bias_down = mlp_parts
    normal_two, inv_two = norm_forward(middle)
    normed_two = (normal_two * gain_two.astype(jnp.float32) + shift_two.astype(jnp.float32)).astype(
        jnp.bfloat16
    )
    hidden_pre = jnp.dot(normed_two, up_full, preferred_element_type=jnp.float32) + bias_up.astype(
        jnp.float32
    )
    activated, slope = gelu_pair(hidden_pre)
    activated = activated.astype(jnp.bfloat16)
    mlp_out = jnp.dot(activated, down_full, preferred_element_type=jnp.float32) + bias_down.astype(
        jnp.float32
    )
    result = (middle + mlp_out).astype(jnp.bfloat16).reshape(tokens.shape)
    valid = (jnp.arange(context)[None, :] < lengths[:, None]).astype(jnp.float32).reshape(-1, 1)
    grad_out = cotangent.reshape(-1, width).astype(jnp.float32) * valid
    mlp_back = (
        lax.all_gather(ln2_gain, "fsdp", axis=0, tiled=True),
        lax.all_gather(ln2_bias, "fsdp", axis=0, tiled=True),
        lax.all_gather(w_up, "fsdp", axis=0, tiled=True),
        lax.all_gather(b_up, "fsdp", axis=0, tiled=True),
        lax.all_gather(w_down, "fsdp", axis=0, tiled=True),
        lax.all_gather(b_down, "fsdp", axis=0, tiled=True),
    )
    gain_two_back, unused_two, up_back, unused_up, down_back, unused_down = mlp_back
    grad_mlp = grad_out.astype(jnp.bfloat16)
    grad_down = jnp.einsum("rf,rd->fd", activated, grad_mlp, preferred_element_type=jnp.float32)
    grad_bias_down = jnp.sum(grad_mlp.astype(jnp.float32), axis=0)
    grad_act = jnp.einsum("rd,fd->rf", grad_mlp, down_back, preferred_element_type=jnp.float32)
    grad_hidden = (grad_act * slope).astype(jnp.bfloat16)
    grad_up = jnp.einsum("rd,rf->df", normed_two, grad_hidden, preferred_element_type=jnp.float32)
    grad_bias_up = jnp.sum(grad_hidden.astype(jnp.float32), axis=0)
    grad_normed_two = jnp.einsum(
        "rf,df->rd", grad_hidden, up_back, preferred_element_type=jnp.float32
    )
    grad_gain_two = jnp.sum(grad_normed_two * normal_two, axis=0)
    grad_shift_two = jnp.sum(grad_normed_two, axis=0)
    grad_middle = grad_out + norm_backward(
        grad_normed_two, normal_two, inv_two, gain_two_back.astype(jnp.float32)
    )
    mlp_rows = (
        lax.psum_scatter(
            grad_gain_two.astype(jnp.bfloat16), "fsdp", scatter_dimension=0, tiled=True
        ).astype(jnp.float32),
        lax.psum_scatter(
            grad_shift_two.astype(jnp.bfloat16), "fsdp", scatter_dimension=0, tiled=True
        ).astype(jnp.float32),
        lax.psum_scatter(
            grad_up.astype(jnp.bfloat16), "fsdp", scatter_dimension=0, tiled=True
        ).astype(jnp.float32),
        lax.psum_scatter(
            grad_bias_up.astype(jnp.bfloat16), "fsdp", scatter_dimension=0, tiled=True
        ).astype(jnp.float32),
        lax.psum_scatter(
            grad_down.astype(jnp.bfloat16), "fsdp", scatter_dimension=0, tiled=True
        ).astype(jnp.float32),
        lax.psum_scatter(
            grad_bias_down.astype(jnp.bfloat16), "fsdp", scatter_dimension=0, tiled=True
        ).astype(jnp.float32),
    )
    row_gain_two, row_shift_two, row_up, row_bias_up, row_down, row_bias_down = mlp_rows
    mlp_sums = (
        lax.psum(row_gain_two.astype(jnp.bfloat16), "dp").astype(jnp.float32),
        lax.psum(row_shift_two.astype(jnp.bfloat16), "dp").astype(jnp.float32),
        lax.psum(row_up.astype(jnp.bfloat16), "dp").astype(jnp.float32),
        lax.psum(row_bias_up.astype(jnp.bfloat16), "dp").astype(jnp.float32),
        lax.psum(row_down.astype(jnp.bfloat16), "dp").astype(jnp.float32),
        lax.psum(row_bias_down.astype(jnp.bfloat16), "dp").astype(jnp.float32),
    )
    attn_back = (
        lax.all_gather(ln1_gain, "fsdp", axis=0, tiled=True),
        lax.all_gather(ln1_bias, "fsdp", axis=0, tiled=True),
        lax.all_gather(w_qkv, "fsdp", axis=0, tiled=True),
        lax.all_gather(b_query, "fsdp", axis=0, tiled=True),
        lax.all_gather(b_value, "fsdp", axis=0, tiled=True),
        lax.all_gather(w_out, "fsdp", axis=0, tiled=True),
        lax.all_gather(b_out, "fsdp", axis=0, tiled=True),
    )
    gain_one_back, unused_shift, qkv_back, unused_query, unused_value, out_back, unused_out = (
        attn_back
    )
    grad_branch = grad_middle.astype(jnp.bfloat16)
    grad_out_proj = jnp.einsum(
        "rd,re->de", attended, grad_branch, preferred_element_type=jnp.float32
    )
    grad_bias_out = jnp.sum(grad_branch.astype(jnp.float32), axis=0)
    grad_attended = jnp.einsum(
        "re,de->rd", grad_branch, out_back, preferred_element_type=jnp.float32
    ).astype(jnp.bfloat16)
    grad_heads = split_heads(grad_attended, seqs, context, heads)
    grad_query_heads, grad_key_heads, grad_value_heads = lax.map(
        partial(head_backward, allowed),
        (query_heads, key_heads, value_heads, grad_heads, log_totals),
    )
    grad_queries = (join_heads(grad_query_heads) * scale).astype(jnp.bfloat16)
    grad_keys = join_heads(grad_key_heads).astype(jnp.bfloat16)
    grad_values = join_heads(grad_value_heads).astype(jnp.bfloat16)
    grad_projected = jnp.concatenate([grad_queries, grad_keys, grad_values], axis=1)
    grad_qkv = jnp.einsum(
        "rd,re->de", normed_one, grad_projected, preferred_element_type=jnp.float32
    )
    grad_bias_query = jnp.sum(grad_queries.astype(jnp.float32), axis=0)
    grad_bias_value = jnp.sum(grad_values.astype(jnp.float32), axis=0)
    grad_normed_one = jnp.einsum(
        "re,de->rd", grad_projected, qkv_back, preferred_element_type=jnp.float32
    )
    grad_gain_one = jnp.sum(grad_normed_one * normal_one, axis=0)
    grad_shift_one = jnp.sum(grad_normed_one, axis=0)
    grad_inputs = grad_middle + norm_backward(
        grad_normed_one, normal_one, inv_one, gain_one_back.astype(jnp.float32)
    )
    attn_rows = (
        lax.psum_scatter(
            grad_gain_one.astype(jnp.bfloat16), "fsdp", scatter_dimension=0, tiled=True
        ).astype(jnp.float32),
        lax.psum_scatter(
            grad_shift_one.astype(jnp.bfloat16), "fsdp", scatter_dimension=0, tiled=True
        ).astype(jnp.float32),
        lax.psum_scatter(
            grad_qkv.astype(jnp.bfloat16), "fsdp", scatter_dimension=0, tiled=True
        ).astype(jnp.float32),
        lax.psum_scatter(
            grad_bias_query.astype(jnp.bfloat16), "fsdp", scatter_dimension=0, tiled=True
        ).astype(jnp.float32),
        lax.psum_scatter(
            grad_bias_value.astype(jnp.bfloat16), "fsdp", scatter_dimension=0, tiled=True
        ).astype(jnp.float32),
        lax.psum_scatter(
            grad_out_proj.astype(jnp.bfloat16), "fsdp", scatter_dimension=0, tiled=True
        ).astype(jnp.float32),
        lax.psum_scatter(
            grad_bias_out.astype(jnp.bfloat16), "fsdp", scatter_dimension=0, tiled=True
        ).astype(jnp.float32),
    )
    row_gain_one, row_shift_one, row_qkv, row_query, row_value, row_out, row_bias_out = attn_rows
    attn_sums = (
        lax.psum(row_gain_one.astype(jnp.bfloat16), "dp").astype(jnp.float32),
        lax.psum(row_shift_one.astype(jnp.bfloat16), "dp").astype(jnp.float32),
        lax.psum(row_qkv.astype(jnp.bfloat16), "dp").astype(jnp.float32),
        lax.psum(row_query.astype(jnp.bfloat16), "dp").astype(jnp.float32),
        lax.psum(row_value.astype(jnp.bfloat16), "dp").astype(jnp.float32),
        lax.psum(row_out.astype(jnp.bfloat16), "dp").astype(jnp.float32),
        lax.psum(row_bias_out.astype(jnp.bfloat16), "dp").astype(jnp.float32),
    )
    return (
        result,
        grad_inputs.reshape(tokens.shape),
        attn_sums[0],
        attn_sums[1],
        attn_sums[2],
        attn_sums[3],
        attn_sums[4],
        attn_sums[5],
        attn_sums[6],
        mlp_sums[0],
        mlp_sums[1],
        mlp_sums[2],
        mlp_sums[3],
        mlp_sums[4],
        mlp_sums[5],
    )


def solution(mesh):
    in_specs = (
        P(("dp", "fsdp"), None, None),
        P(("dp", "fsdp")),
        P(("dp", "fsdp"), None),
        P(("dp", "fsdp"), None, None),
        P("fsdp"),
        P("fsdp"),
        P("fsdp", None),
        P("fsdp"),
        P("fsdp"),
        P("fsdp", None),
        P("fsdp"),
        P("fsdp"),
        P("fsdp"),
        P("fsdp", None),
        P("fsdp"),
        P("fsdp", None),
        P("fsdp"),
    )
    out_specs = (
        P(("dp", "fsdp"), None, None),
        P(("dp", "fsdp"), None, None),
        P("fsdp"),
        P("fsdp"),
        P("fsdp", None),
        P("fsdp"),
        P("fsdp"),
        P("fsdp", None),
        P("fsdp"),
        P("fsdp"),
        P("fsdp"),
        P("fsdp", None),
        P("fsdp"),
        P("fsdp", None),
        P("fsdp"),
    )
    return jax.shard_map(
        per_device, mesh=mesh, in_specs=in_specs, out_specs=out_specs, check_vma=False
    )
```

profile of v0, /device:TPU:0, one launch (start us, length us, event | category | flops | bytes accessed | tf_op | source)
XLA Modules:
  0.0 642.1 jit_solution(9640326640721068901)
XLA Ops:
  14.4 32.5 %all-reduce.18 = (bf16[768]{0:T(1024)(128)(2,1)S(1)}, bf16[768]{0:T(1024)(128)(2,1)S(1)}, bf16[768]{0:T(1024)(128)(2,1)S(1)}, bf16[768]{0:T(1024)(128)(2,1)S(1)}...) all-reduce(bf16[768]{0:T(1024)(128)(2,1)S(1)} %dynamic-update-slice, ...), channel_id=1, replica_groups=mesh['dp'=4,'fsdp'=8] {'fsdp'}, use_global_device_ids=true, to_apply=%add.1 | all-reduce | flops 5376 | bytes 21504
  52.8 12.7 %all-gather = bf16[8,1,384]{2,1,0:T(2,128)(2,1)S(1)} all-gather(bf16[1,1,384]{2,1,0:T(2,128)(2,1)S(1)} %reshape.386), channel_id=1, replica_groups=mesh['dp'=4,'fsdp'=8] {'fsdp'}, dimensions={0}, use_global_device_ids=true | all-gather | bytes 6912 | tf_op jit(solution)/shard_map/all_gather | solution.py:156
  65.7 6.3 fusion.98
  87.1 69.4 %while.30 = (s32[]{:T(128)}, bf16[12,1,1024,64]{2,3,1,0:T(8,128)(2,1)S(1)}, f32[12,1,1024]{2,1,0:T(1,128)S(1)}, bf16[12,1,1024,64]{3,2,1,0:T(8,128)(2,1)}, bf16[...) while((s32[]{:T(128)}, ...), condition=%wide.region_5.6_spmd.clone.clone, body=%wide.region_2.5_spmd.clone.sunk.clone | while | flops 281017344 | bytes 13676633 | solution.py:143
  157.7 3.9 fusion.106
  162.0 10.7 %fusion.100 = f32[1024,3072]{1,0:T(8,128)} fusion(bf16[768,3072]{1,0:T(8,128)(2,1)} %all-gather.10.cloned.1.call-done, f32[1024,768]{0,1:T(8,128)S(1)} %get-tuple-element.332, f32[768]{0:T(1024)S(1)} %convert_element_type.246, f32[768]{0:T(1024)S(1)} %convert_element_type.245, f32[1024]{0:T(1024)S(1)} %add_rsqrt_fusion, f32[1024]{0:T(1024)S(1)} %broadcast_multiply_fusion.4), kind=kOutput, calls=%fused_computation.139 | convolution fusion | flops 4835770368 | bytes 20461568 | tf_op jit(solution)/shard_map/dot_general | solution.py:165
  172.6 9.1 %all-gather.12.cloned.1.call-done = bf16[3072,768]{1,0:T(8,128)(2,1)} async-done(((bf16[384,768]{1,0:T(8,128)(2,1)}), bf16[3072,768]{1,0:T(8,128)(2,1)}) %all-gather.12.cloned.1.call-update) | async-done | bytes 4718608 | tf_op jit(solution)/shard_map/all_gather | solution.py:157
  181.7 16.5 %fusion.109 = (bf16[3072]{0:T(1024)(128)(2,1)S(1)}, bf16[1024,3072]{1,0:T(8,128)(2,1)S(1)}) fusion(f32[1024,3072]{1,0:T(8,128)} %fusion.100, f32[3072]{0:T(1024)S(1)} %bitcast.226, bf16[3072,768]{1,0:T(8,128)(2,1)} %all-gather.12.cloned.1.call-done, bf16[1,1024,768]{1,2,0:T(8,128)(2,1)} %copy.72, f32[1024]{0:T(1024)S(1)} %fusion.92), kind=kOutput, calls=%fused_computation.147 | convolution fusion | flops 4900254720 | bytes 25188352 | tf_op jit(solution)/shard_map/rd,fd->rf/dot_general | solution.py:188
  198.3 6.7 %fusion.108 = (bf16[768]{0:T(1024)(128)(2,1)S(1)}, f32[1024,768]{1,0:T(8,128)}) fusion(bf16[1024,3072]{1,0:T(8,128)(2,1)S(1)} %get-tuple-element.338, bf16[768,3072]{1,0:T(8,128)(2,1)S(1)} %copy-done.12), kind=kOutput, calls=%fused_computation.146 | convolution fusion | flops 4832623616 | bytes 14157312 | tf_op jit(solution)/shard_map/rf,df->rd/dot_general | solution.py:192
  217.8 4.8 convolution_convert_fusion.3
  222.6 4.3 copy.74
  226.9 171.0 %while.31 = (s32[]{:T(128)}, f32[12,1,1024,64]{2,3,1,0:T(8,128)}, bf16[12,1,1024,64]{2,3,1,0:T(8,128)(2,1)}, bf16[12,1,1024,64]{2,3,1,0:T(8,128)(2,1)}, bf16[12,...) while((s32[]{:T(128)}, f32[12,1,1024,64]{2,3,1,0:T(8,128)}, ...), condition=%wide.region_12.13_spmd.clone.clone, body=%wide.region_10.12_spmd.clone.sunk.clone | while | flops 684719104 | bytes 46689448 | solution.py:250
  228.6 3.8 multiply_reduce_fusion.8
  242.9 3.8 multiply_reduce_fusion.8
  271.4 3.8 multiply_reduce_fusion.8
  285.6 3.8 multiply_reduce_fusion.8
  314.1 3.8 multiply_reduce_fusion.8
  328.4 3.8 multiply_reduce_fusion.8
  342.6 3.8 multiply_reduce_fusion.8
  356.9 3.8 multiply_reduce_fusion.8
  371.1 3.8 multiply_reduce_fusion.8
  385.3 3.8 multiply_reduce_fusion.8
  401.5 7.3 %convolution_convert_fusion.2 = bf16[768,2304]{1,0:T(8,128)(2,1)} fusion(bf16[1024,768]{0,1:T(8,128)(2,1)} %bitcast.24, bf16[1024,768]{0,1:T(8,128)(2,1)S(1)} %bitcast.214, bf16[1024,768]{0,1:T(8,128)(2,1)S(1)} %bitcast.221, bf16[1,1024,768]{1,2,0:T(8,128)(2,1)S(1)} %copy-done.1, f32[768]{0:T(1024)S(1)} %copy-done.24, f32[768]{0:T(1024)S(1)} %copy-done.19, ...), kind=kOutput, calls=%fused_computation.77 | convolution fusion | flops 3644522496 | bytes 9844736 | tf_op jit(solution)/shard_map/rd,re->de/dot_general | solution.py:258
  408.8 9.7 %convolution_convert_fusion.1 = bf16[768,3072]{1,0:T(8,128)(2,1)} fusion(bf16[1024,3072]{1,0:T(8,128)(2,1)} %copy-done.35, f32[1024,768]{0,1:T(8,128)S(1)} %get-tuple-element.332, f32[768]{0:T(1024)S(1)} %convert_element_type.246, f32[768]{0:T(1024)S(1)} %convert_element_type.245, f32[1024]{0:T(1024)S(1)} %add_rsqrt_fusion, ...), kind=kOutput, calls=%fused_computation.76 | convolution fusion | flops 4838129664 | bytes 14170112 | tf_op jit(solution)/shard_map/rd,rf->df/dot_general | solution.py:190
  418.6 13.9 %convolution_convert_fusion = bf16[3072,768]{1,0:T(8,128)(2,1)} fusion(bf16[1,1024,768]{1,2,0:T(8,128)(2,1)} %copy.72, f32[1024]{0:T(1024)S(1)} %fusion.92, f32[1024,3072]{1,0:T(8,128)} %fusion.100, f32[3072]{0:T(1024)S(1)} %bitcast.227), kind=kOutput, calls=%fused_computation.75 | convolution fusion | flops 4868014080 | bytes 18890752 | tf_op jit(solution)/shard_map/rf,rd->fd/dot_general | solution.py:186
  434.1 9.1 %fusion.107 = (bf16[768]{0:T(1024)(128)(2,1)S(1)}, f32[1024,768]{1,0:T(8,128)}) fusion(bf16[768,2304]{1,0:T(8,128)(2,1)} %all-gather.6.cloned.1.call-done, bf16[1024,768]{0,1:T(8,128)(2,1)} %bitcast.24, bf16[1024,768]{0,1:T(8,128)(2,1)} %bitcast.213, bf16[1024,768]{0,1:T(8,128)(2,1)} %bitcast.222), kind=kOutput, calls=%fused_computation.145 | convolution fusion | flops 3638820096 | bytes 11404800 | tf_op jit(solution)/shard_map/re,de->rd/dot_general | solution.py:263
  452.1 28.3 %all-reduce.17 = (bf16[768]{0:T(1024)(128)(2,1)S(1)}, bf16[768]{0:T(1024)(128)(2,1)S(1)}, bf16[768]{0:T(1024)(128)(2,1)S(1)}, bf16[768]{0:T(1024)(128)(2,1)S(1)}...) all-reduce(bf16[768]{0:T(1024)(128)(2,1)S(1)} %dynamic-update-slice, ...), channel_id=1, replica_groups=mesh['dp'=4,'fsdp'=8] {'fsdp'}, use_global_device_ids=true, to_apply=%add.7 | all-reduce | flops 9984 | bytes 39936
  481.1 10.0 %all-reduce.19 = (bf16[96]{0:T(256)(128)(2,1)S(1)}, bf16[96]{0:T(256)(128)(2,1)S(1)}, bf16[96]{0:T(256)(128)(2,1)S(1)}, bf16[96]{0:T(256)(128)(2,1)S(1)}, bf16[9...) all-reduce(bf16[96]{0:T(256)(128)(2,1)S(1)} %dynamic-slice.9, ...), channel_id=1, replica_groups=mesh['dp'=4,'fsdp'=8] {'dp'}, use_global_device_ids=true, to_apply=%region_17.18 | all-reduce | flops 1152 | bytes 4608 | tf_op jit(solution)/shard_map/psum | solution.py:296
  495.7 6.0 fusion.78
  507.6 55.4 %reduce-scatter.11.cloned.1.call-done = bf16[384,768]{1,0:T(8,128)(2,1)} async-done(((bf16[3072,768]{1,0:T(8,128)(2,1)}), bf16[384,768]{1,0:T(8,128)(2,1)}) %reduce-scatter.11.cloned.1.call-update) | async-done | bytes 589840 | tf_op jit(solution)/shard_map/reduce_scatter | solution.py:213
  562.9 11.6 %fusion.88 = bf16[1,1024,768]{1,2,0:T(8,128)(2,1)} fusion(f32[1024,768]{0,1:T(8,128)S(1)} %get-tuple-element.332, f32[768]{0:T(1024)S(1)} %convert_element_type.250, bf16[3072,768]{1,0:T(8,128)(2,1)} %all-gather.12.cloned.1.call-done, f32[1024,3072]{1,0:T(8,128)} %fusion.100, f32[3072]{0:T(1024)S(1)} %bitcast.228), kind=kOutput, calls=%fused_computation.120 | convolution fusion | flops 4865654784 | bytes 22035456 | tf_op jit(solution)/shard_map/dot_general | solution.py:170
  577.1 51.9 %all-reduce.23.cloned.1.call-done = (bf16[96,2304]{1,0:T(8,128)(2,1)}, bf16[96,768]{1,0:T(8,128)(2,1)}, bf16[96,3072]{1,0:T(8,128)(2,1)}, bf16[384,768]{1,0:T(8,128)(2,1)}) async-done(((bf16[96,2304]{1,0:T(8,128)(2,1)}, bf16[96,768]{1,0:T(8,128)(2,1)}, bf16[96,3072]{1,0:T(8,128)(2,1)}, bf16[384,768]{1,0:T(8,128)(2,1)}), (bf16[96,2304]{1,0:T(8,128)(2,1)}, bf16[96,768]{1,0:T(8,128)(2,1)}, ...) | async-done | bytes 1769488 | tf_op jit(solution)/shard_map/psum | solution.py:298
  (362 shorter events, 275.5 us)
Async XLA Ops:
  7.2 58.5 %all-gather.6.cloned.1.call-start = ((), (), s32[]{:S(2)}) async-start(), calls=%async_computation.4 | async-start | bytes 3981312 | tf_op jit(solution)/shard_map/all_gather | solution.py:123
  7.9 148.7 %all-gather.8.cloned.1.call-start = ((), (), s32[]{:S(2)}) async-start(), calls=%async_computation.5 | async-start | bytes 1327104 | tf_op jit(solution)/shard_map/all_gather | solution.py:126
  8.7 153.3 %all-gather.10.cloned.1.call-start = ((), (), s32[]{:S(2)}) async-start(), calls=%async_computation.6 | async-start | bytes 5308416 | tf_op jit(solution)/shard_map/all_gather | solution.py:155
  9.4 172.3 %all-gather.12.cloned.1.call-start = ((), (), s32[]{:S(2)}) async-start(), calls=%async_computation.7 | async-start | bytes 5308416 | tf_op jit(solution)/shard_map/all_gather | solution.py:157
  10.0 495.4 %reduce-scatter.7.cloned.1.call-start = ((), (), s32[]{:S(2)}) async-start(), calls=%async_computation.9 | async-start | bytes 1327104 | tf_op jit(solution)/shard_map/reduce_scatter | solution.py:287
  10.2 61.7 %copy-start.3 = (bf16[12,1,1024,64]{2,3,1,0:T(8,128)(2,1)}, bf16[12,1,1024,64]{2,3,1,0:T(8,128)(2,1)S(1)}, u32[]{:S(2)}) copy-start(bf16[12,1,1024,64]{2,3,1,0:T(8,128)(2,1)S(1)} %fusion.104) | copy-start | bytes 4718596
  10.3 3.4 copy-start.31
  10.3 3.6 copy-start.32
  10.3 3.9 copy-start.33
  46.9 18.7 %copy-start.18 = (f32[768]{0:T(1024)}, f32[768]{0:T(1024)S(1)}, u32[]{:S(2)}) copy-start(f32[768]{0:T(1024)S(1)} %convert_element_type.234) | copy-start | bytes 9220
  46.9 18.8 %copy-start.23 = (f32[768]{0:T(1024)}, f32[768]{0:T(1024)S(1)}, u32[]{:S(2)}) copy-start(f32[768]{0:T(1024)S(1)} %convert_element_type.235) | copy-start | bytes 9220
  46.9 3.2 copy-start.22
  48.6 17.0 %copy-start = (bf16[1,1024,768]{1,2,0:T(8,128)(2,1)}, bf16[1,1024,768]{1,2,0:T(8,128)(2,1)S(1)}, u32[]{:S(2)}) copy-start(bf16[1,1024,768]{1,2,0:T(8,128)(2,1)S(1)} %copy.64) | copy-start | bytes 4718596
  48.6 4.2 copy-start.26
  48.9 23.0 %copy-start.16 = (f32[1024]{0:T(1024)}, f32[1024]{0:T(1024)S(1)}, u32[]{:S(2)}) copy-start(f32[1024]{0:T(1024)S(1)} %broadcast_multiply_fusion.5) | copy-start | bytes 12292
  49.4 22.6 %copy-start.20 = (f32[1024]{0:T(1024)}, f32[1024]{0:T(1024)S(1)}, u32[]{:S(2)}) copy-start(f32[1024]{0:T(1024)S(1)} %add_rsqrt_fusion.1) | copy-start | bytes 12292
  181.7 16.5 %copy-start.12 = (bf16[768,3072]{1,0:T(8,128)(2,1)S(1)}, bf16[768,3072]{1,0:T(8,128)(2,1)}, u32[]{:S(2)}) copy-start(bf16[768,3072]{1,0:T(8,128)(2,1)} %all-gather.10.cloned.1.call-done) | copy-start | bytes 14155780
  198.3 6.8 %copy-start.35 = (bf16[1024,3072]{1,0:T(8,128)(2,1)}, bf16[1024,3072]{1,0:T(8,128)(2,1)S(1)}, u32[]{:S(2)}) copy-start(bf16[1024,3072]{1,0:T(8,128)(2,1)S(1)} %get-tuple-element.338) | copy-start | bytes 18874372
  208.6 3.3 copy-start.11
  211.9 3.4 copy-start.8
  217.7 287.6 %reduce-scatter.5.cloned.1.call-start = ((), (), s32[]{:S(2)}) async-start(), calls=%async_computation.8 | async-start | bytes 3981312 | tf_op jit(solution)/shard_map/reduce_scatter | solution.py:278
  397.8 3.6 copy-start.1
  397.8 3.6 copy-start.6
  397.8 3.6 copy-start.17
  397.8 3.6 copy-start.19
  397.9 3.6 copy-start.21
  397.9 3.6 copy-start.24
  408.8 98.8 %reduce-scatter.9.cloned.1.call-start = ((), (), s32[]{:S(2)}) async-start(), calls=%async_computation.10 | async-start | bytes 5308416 | tf_op jit(solution)/shard_map/reduce_scatter | solution.py:207
  418.6 144.3 %reduce-scatter.11.cloned.1.call-start = ((), (), s32[]{:S(2)}) async-start(), calls=%async_computation.11 | async-start | bytes 5308416 | tf_op jit(solution)/shard_map/reduce_scatter | solution.py:213
  432.5 196.5 %all-reduce.23.cloned.1.call-start = ((), (), s32[]{:S(2)}) async-start(), calls=%async_computation.12 | async-start | bytes 3538944 | tf_op jit(solution)/shard_map/psum | solution.py:298
  629.0 4.4 copy-start.14
  629.0 5.4 copy-start.15
  (35 other events, 65.6 us)
Sparse Core Ops, SparseCore 0:
  9.6 44.6 all-gather.5
  56.0 21.6 all-gather.7
  79.3 50.8 all-gather.9
  131.7 49.9 all-gather.11
  217.8 31.6 reduce-scatter.6
  408.9 42.4 reduce-scatter.4
  453.7 53.8 reduce-scatter.8
  509.9 53.0 reduce-scatter.10
  566.4 62.6 all-reduce.22
where the time goes:
time: 652 us; the launch traced here: 642 us
  matrix products  307 us (47%)
  waiting for transfers between devices  121 us (19%)
  blocking collectives  83.5 us (13%)
  local copies, waits for them, and re-layouts  57.5 us (9%)
  other arithmetic  54 us (8%)
  between operations  17.4 us (3%)
    unnamed x2, blocking collectives  60.8 us
    reduce_scatter x1, waiting for transfers between devices, per_device(): lax.psum_scatter(grad_down.astype(jnp.bfloat16), 'fsdp', scatter_dimensio...  55.4 us
    psum x1, waiting for transfers between devices, per_device(): lax.psum(row_qkv.astype(jnp.bfloat16), 'dp').astype(jnp.float32)  51.9 us
    dot_general x12, matrix products, head_backward(): jnp.einsum('sqd,skd->sqk', query_head, key_head, preferred_element_type=j...  45.3 us
    dot_general x12, matrix products, head_forward(): jnp.einsum('sqd,skd->sqk', query_head, key_head, preferred_element_type=j...  39.4 us
    dot_general x12, matrix products, head_backward(): jnp.einsum('sqk,sqd->skd', softmax_rows.astype(jnp.bfloat16), grad_head,...  28.5 us
    dot_general x12, matrix products, head_backward(): jnp.einsum('sqk,skd->sqd', grad_scores, key_head, preferred_element_type=...  27.8 us
    unnamed x103, local copies, waits for them, and re-layouts  27.4 us
  transfers between devices with their start and end apart: 9, of which 4 were waited for; matrix products, arithmetic and copies ran while one was open for 56% of the time, Pallas kernels for 0%

commit v1 on v0

v1 whole, which is shorter than its diff:
```python
from functools import partial
import math

import jax
import jax.numpy as jnp
from jax import lax
from jax.experimental import pallas as pl
from jax.experimental.pallas import tpu as pltpu
from jax.sharding import PartitionSpec as P

HEADS = 12
EPSILON = 1e-05
GELU_C = 0.7978845608028654
GELU_A = 0.044715
MASKED = -1e30
TILE = 256
VMEM_BYTES = 60 * 1024 * 1024
F32 = jnp.float32
BF16 = jnp.bfloat16


def mm(a, b):
    return jnp.dot(a, b, preferred_element_type=F32)


def mm_nt(a, b):
    return lax.dot_general(a, b, (((1,), (1,)), ((), ())), preferred_element_type=F32)


def mm_tn(a, b):
    return lax.dot_general(a, b, (((0,), (0,)), ((), ())), preferred_element_type=F32)


def params(**kw):
    return pltpu.CompilerParams(
        dimension_semantics=("arbitrary",), vmem_limit_bytes=VMEM_BYTES, **kw
    )


def cost(flops, bytes_accessed, transcendentals=0):
    return pl.CostEstimate(
        flops=int(flops), bytes_accessed=int(bytes_accessed), transcendentals=int(transcendentals)
    )


def norm_forward(values):
    row_mean = jnp.mean(values, axis=-1, keepdims=True)
    centered = values - row_mean
    inv_std = lax.rsqrt(jnp.mean(centered * centered, axis=-1, keepdims=True) + EPSILON)
    return centered * inv_std, inv_std


def norm_backward(grad_normed, normalized, inv_std, gain):
    scaled = grad_normed * gain
    return inv_std * (
        scaled
        - jnp.mean(scaled, axis=-1, keepdims=True)
        - normalized * jnp.mean(scaled * normalized, axis=-1, keepdims=True)
    )


def gelu_pair(u):
    square = u * u
    tanh_part = jnp.tanh(u * (GELU_C + (GELU_C * GELU_A) * square))
    half = 0.5 + 0.5 * tanh_part
    value = u * half
    slope = half + value * (1.0 - tanh_part) * (GELU_C + (3.0 * GELU_C * GELU_A) * square)
    return value, slope


def whole(shape):
    return pl.BlockSpec(shape, lambda i: (0,) * len(shape), pipeline_mode=pl.Buffered(1))


def rows_spec(tile, width):
    return pl.BlockSpec((tile, width), lambda i: (i, 0))


def qkv_kernel(scale, x_ref, w_ref, gain_ref, shift_ref, bq_ref, bv_ref, a1_ref, qkv_ref):
    width = x_ref.shape[1]
    xhat, _ = norm_forward(x_ref[...].astype(F32))
    a1 = (xhat * gain_ref[...] + shift_ref[...]).astype(BF16)
    a1_ref[...] = a1
    q = mm(a1, w_ref[:, 0:width])
    qkv_ref[:, 0:width] = ((q + bq_ref[...]) * scale).astype(BF16)
    k = mm(a1, w_ref[:, width : 2 * width])
    qkv_ref[:, width : 2 * width] = k.astype(BF16)
    v = mm(a1, w_ref[:, 2 * width : 3 * width])
    qkv_ref[:, 2 * width : 3 * width] = (v + bv_ref[...]).astype(BF16)


def qkv_forward(x, w_qkv, gain, shift, bq, bv, scale):
    rows, width = x.shape
    vec = whole((1, width))
    return pl.pallas_call(
        partial(qkv_kernel, scale),
        grid=(rows // TILE,),
        in_specs=[rows_spec(TILE, width), whole(w_qkv.shape), vec, vec, vec, vec],
        out_specs=[rows_spec(TILE, width), rows_spec(TILE, 3 * width)],
        out_shape=[
            jax.ShapeDtypeStruct((rows, width), BF16),
            jax.ShapeDtypeStruct((rows, 3 * width), BF16),
        ],
        compiler_params=params(),
        cost_estimate=cost(6 * rows * width * width, 12 * rows * width),
        name="qkv_forward",
    )(x, w_qkv, gain, shift, bq, bv)


def split3(value):
    first = value.astype(BF16)
    rest = value - first.astype(F32)
    second = rest.astype(BF16)
    third = (rest - second.astype(F32)).astype(BF16)
    return first, second, third


def attn_fwd_kernel(q_ref, k_ref, v_ref, kbias_ref, rbias_ref, o_ref, qa_ref, mask_ref):
    blocks = q_ref.shape[0] // TILE
    lane = lax.broadcasted_iota(jnp.int32, (1, 128), 1)

    @pl.when(pl.program_id(0) == 0)
    def _():
        row = lax.broadcasted_iota(jnp.int32, (TILE, TILE), 0)
        col = lax.broadcasted_iota(jnp.int32, (TILE, TILE), 1)
        for i in range(blocks):
            usable = rbias_ref[:, i * TILE : (i + 1) * TILE]
            mask_ref[i] = jnp.where(row == col, 0.0, jnp.where(row > col, usable, MASKED))

    zero = jnp.zeros((), BF16)
    one = jnp.ones((), BF16)
    for head in range(2):
        base = 64 * head
        extra = 64 - base
        own = (lane >= base) & (lane < base + 64)
        k_off = jnp.where(own, k_ref[...], jnp.where(lane == extra, kbias_ref[...], zero))
        for i in range(blocks):
            here = slice(i * TILE, (i + 1) * TILE)
            q = jnp.where(own, q_ref[here, :], zero)
            q_off = jnp.where(lane == extra, one, q)
            s_diag = mm_nt(q, k_ref[here, :]) + mask_ref[i]
            row_max = jnp.max(s_diag, axis=-1, keepdims=True)
            if i:
                s_off = mm_nt(q_off, k_off[: i * TILE])
                row_max = jnp.maximum(row_max, jnp.max(s_off, axis=-1, keepdims=True))
            e_diag = jnp.exp(s_diag - row_max)
            total = jnp.sum(e_diag, axis=-1, keepdims=True)
            o = mm(e_diag.astype(BF16), v_ref[here, :])
            if i:
                e_off = jnp.exp(s_off - row_max)
                total += jnp.sum(e_off, axis=-1, keepdims=True)
                o += mm(e_off.astype(BF16), v_ref[0 : i * TILE, :])
            o = (o * (1.0 / total)).astype(BF16)
            if head:
                o_ref[here, :] = jnp.where(own, o, o_ref[here, :])
            else:
                o_ref[here, :] = o
            first, second, third = split3(-(row_max + jnp.log(total)))
            qa = jnp.where(lane == extra + 1, first, q_off)
            qa = jnp.where(lane == extra + 2, second, qa)
            qa = jnp.where(lane == extra + 3, third, qa)
            qa_ref[here, 128 * head : 128 * head + 128] = qa


def attn_forward(qkv, kbias, rbias):
    rows = qkv.shape[0]
    width = qkv.shape[1] // 3
    pairs = width // 128

    def part(p):
        return pl.BlockSpec((rows, 128), lambda i: (0, p * pairs + i))

    return pl.pallas_call(
        attn_fwd_kernel,
        grid=(pairs,),
        in_specs=[part(0), part(1), part(2), whole(kbias.shape), whole(rbias.shape)],
        out_specs=[part(0), pl.BlockSpec((rows, 256), lambda i: (0, i))],
        out_shape=[
            jax.ShapeDtypeStruct((rows, width), BF16),
            jax.ShapeDtypeStruct((rows, 2 * width), BF16),
        ],
        scratch_shapes=[pltpu.VMEM((rows // TILE, TILE, TILE), F32)],
        compiler_params=params(),
        cost_estimate=cost(8 * rows * rows * width, 12 * rows * width),
        name="attn_forward",
    )(qkv, qkv, qkv, kbias, rbias)


def attn_bwd_kernel(
    qa_ref, k_ref, v_ref, o_ref, do_ref, kbias_ref, dq_ref, dk_ref, dv_ref, mask_ref, doa_ref, dqt_ref
):
    rows = k_ref.shape[0]
    blocks = rows // TILE
    lane = lax.broadcasted_iota(jnp.int32, (1, 128), 1)

    @pl.when(pl.program_id(0) == 0)
    def _():
        key = lax.broadcasted_iota(jnp.int32, (TILE, TILE), 0)
        query = lax.broadcasted_iota(jnp.int32, (TILE, TILE), 1)
        for i in range(blocks):
            usable = kbias_ref[i * TILE : (i + 1) * TILE, 0:1].astype(F32)
            mask_ref[i] = jnp.where(key == query, 0.0, jnp.where(query > key, usable, MASKED))

    zero = jnp.zeros((), BF16)
    one = jnp.ones((), BF16)
    product = do_ref[...].astype(F32) * o_ref[...].astype(F32)
    kt = k_ref[...].T
    for head in range(2):
        base = 64 * head
        extra = 64 - base
        own = (lane >= base) & (lane < base + 64)
        terms = (lane > extra) & (lane <= extra + 3)
        qa_cols = slice(128 * head, 128 * head + 128)
        inner = -jnp.sum(jnp.where(own, product, 0.0), axis=-1, keepdims=True)
        first, second, third = split3(inner)
        doa = jnp.where(own, do_ref[...], zero)
        doa = jnp.where(lane == extra + 1, first, doa)
        doa = jnp.where(lane == extra + 2, second, doa)
        doa_ref[...] = jnp.where(lane == extra + 3, third, doa)
        for j in range(blocks):
            here = slice(j * TILE, (j + 1) * TILE)
            after = slice((j + 1) * TILE, rows)
            k_diag = jnp.where(own, k_ref[here, :], jnp.where(terms, one, zero))
            v_aug = jnp.where(own, v_ref[here, :], jnp.where(terms, one, zero))
            p_diag = jnp.exp(mm_nt(k_diag, qa_ref[here, qa_cols]) + mask_ref[j])
            dp_diag = mm_nt(v_aug, doa_ref[here, :])
            ds_diag = (p_diag * dp_diag).astype(BF16)
            dv = mm(p_diag.astype(BF16), do_ref[here, :])
            dk = mm(ds_diag, qa_ref[here, qa_cols])
            dq_diag = mm(kt[:, here], ds_diag)
            if j:
                dqt_ref[:, here] += dq_diag
            else:
                dqt_ref[:, here] = dq_diag
            if j + 1 < blocks:
                k_off = jnp.where(lane == extra, kbias_ref[here, :], k_diag)
                p_off = jnp.exp(mm_nt(k_off, qa_ref[after, qa_cols]))
                dp_off = mm_nt(v_aug, doa_ref[after, :])
                ds_off = (p_off * dp_off).astype(BF16)
                dv += mm(p_off.astype(BF16), do_ref[after, :])
                dk += mm(ds_off, qa_ref[after, qa_cols])
                dq_off = mm(kt[:, here], ds_off)
                if j:
                    dqt_ref[:, after] += dq_off
                else:
                    dqt_ref[:, after] = dq_off
            dk = dk.astype(BF16)
            dv = dv.astype(BF16)
            if head:
                dk_ref[here, :] = jnp.where(own, dk, dk_ref[here, :])
                dv_ref[here, :] = jnp.where(own, dv, dv_ref[here, :])
            else:
                dk_ref[here, :] = dk
                dv_ref[here, :] = dv
        dq = (dqt_ref[...] * 0.125).astype(BF16).T
        if head:
            dq_ref[...] = jnp.where(own, dq, dq_ref[...])
        else:
            dq_ref[...] = dq


def attn_backward(qa, qkv, o, do, kbias, first_pair, pair_count):
    rows, width = o.shape
    pairs = width // 128

    def part(p):
        return pl.BlockSpec((rows, 128), lambda i: (0, p * pairs + first_pair + i))

    out = pl.BlockSpec((rows, 128), lambda i: (0, i))
    shape = jax.ShapeDtypeStruct((rows, 128 * pair_count), BF16)
    return pl.pallas_call(
        attn_bwd_kernel,
        grid=(pair_count,),
        in_specs=[
            pl.BlockSpec((rows, 256), lambda i: (0, first_pair + i)),
            part(1),
            part(2),
            part(0),
            part(0),
            whole(kbias.shape),
        ],
        out_specs=[out, out, out],
        out_shape=[shape, shape, shape],
        scratch_shapes=[
            pltpu.VMEM((rows // TILE, TILE, TILE), F32),
            pltpu.VMEM((rows, 128), BF16),
            pltpu.VMEM((128, rows), F32),
        ],
        compiler_params=params(),
        cost_estimate=cost(20 * rows * rows * 128 * pair_count, 18 * rows * 128 * pair_count),
        name="attn_backward",
    )(qa, qkv, qkv, o, do, kbias)


def mlp_kernel(
    x_ref, o_ref, cot_ref, valid_ref, wo_ref, wu_ref, wd_ref, bo_ref, gain_ref, shift_ref, bu_ref, bd_ref,
    out_ref, dm_ref, a2_ref, g_ref, du_ref, dr_ref, dy_ref, do_ref,
    s_gain_ref, s_shift_ref, s_bu_ref, s_bd_ref, s_bo_ref,
):
    chunk = 768
    hidden = wu_ref.shape[1]
    middle = x_ref[...].astype(F32) + mm(o_ref[...], wo_ref[...]) + bo_ref[...]
    xhat, inv_std = norm_forward(middle)
    a2 = (xhat * gain_ref[...] + shift_ref[...]).astype(BF16)
    a2_ref[...] = a2
    dout = cot_ref[...].astype(F32) * valid_ref[:, 0:1]
    dm = dout.astype(BF16)
    dm_ref[...] = dm
    out = middle + bd_ref[...]
    da2 = jnp.zeros_like(middle)
    first = pl.program_id(0) == 0

    def add_sum(ref, cols, value):
        part = jnp.sum(value, axis=0, keepdims=True)
        ref[:, cols] = jnp.where(first, part, ref[:, cols] + part)

    for c in range(hidden // chunk):
        cols = slice(c * chunk, (c + 1) * chunk)
        u = mm(a2, wu_ref[:, cols]) + bu_ref[:, cols]
        value, slope = gelu_pair(u)
        g = value.astype(BF16)
        g_ref[:, cols] = g
        out += mm(g, wd_ref[cols, :])
        du = (mm_nt(dm, wd_ref[cols, :]) * slope).astype(BF16)
        du_ref[:, cols] = du
        add_sum(s_bu_ref, cols, du.astype(F32))
        da2 += mm_nt(du, wu_ref[:, cols])
    out_ref[...] = out.astype(BF16)
    every = slice(None)
    add_sum(s_bd_ref, every, dm.astype(F32))
    add_sum(s_gain_ref, every, da2 * xhat)
    add_sum(s_shift_ref, every, da2)
    dr = dout + norm_backward(da2, xhat, inv_std, gain_ref[...])
    dr_ref[...] = dr
    dy = dr.astype(BF16)
    dy_ref[...] = dy
    add_sum(s_bo_ref, every, dy.astype(F32))
    do_ref[...] = mm_nt(dy, wo_ref[...]).astype(BF16)


def mlp_both(x, o, cot, valid, w_out, w_up, w_down, b_out, gain, shift, b_up, b_down):
    rows, width = x.shape
    hidden = w_up.shape[1]
    row = rows_spec(TILE, width)
    wide = rows_spec(TILE, hidden)
    vec = whole((1, width))
    vec_wide = whole((1, hidden))
    acc = pl.BlockSpec((1, width), lambda i: (0, 0))
    acc_wide = pl.BlockSpec((1, hidden), lambda i: (0, 0))

    def shape(r, c, t):
        return jax.ShapeDtypeStruct((r, c), t)

    return pl.pallas_call(
        mlp_kernel,
        grid=(rows // TILE,),
        in_specs=[
            row, row, row, rows_spec(TILE, 128),
            whole(w_out.shape), whole(w_up.shape), whole(w_down.shape),
            vec, vec, vec, vec_wide, vec,
        ],
        out_specs=[row, row, row, wide, wide, row, row, row, acc, acc, acc_wide, acc, acc],
        out_shape=[
            shape(rows, width, BF16), shape(rows, width, BF16), shape(rows, width, BF16),
            shape(rows, hidden, BF16), shape(rows, hidden, BF16), shape(rows, width, F32),
            shape(rows, width, BF16), shape(rows, width, BF16),
            shape(1, width, F32), shape(1, width, F32), shape(1, hidden, F32),
            shape(1, width, F32), shape(1, width, F32),
        ],
        compiler_params=params(),
        cost_estimate=cost(rows * width * (8 * hidden + 4 * width), 24 * rows * width + 12 * rows * hidden),
        name="mlp_both",
    )(x, o, cot, valid, w_out, w_up, w_down, b_out, gain, shift, b_up, b_down)


def grad_kernel(tall, a_ref, *refs):
    out_ref = refs[-1]
    out_ref[...] = mm_tn(a_ref[...], refs[0][...]).astype(BF16)


def weight_grad(a, b, name):
    rows, m = a.shape
    n = b.shape[1]
    tall = m > n
    tile = 512 if max(m, n) % 512 == 0 else 384
    tile = min(tile, max(m, n))
    if tall:
        specs = [pl.BlockSpec((rows, tile), lambda i: (0, i)), whole(b.shape)]
        out = pl.BlockSpec((tile, n), lambda i: (i, 0))
    else:
        specs = [whole(a.shape), pl.BlockSpec((rows, tile), lambda i: (0, i))]
        out = pl.BlockSpec((m, tile), lambda i: (0, i))
    return pl.pallas_call(
        partial(grad_kernel, tall),
        grid=(max(m, n) // tile,),
        in_specs=specs,
        out_specs=out,
        out_shape=jax.ShapeDtypeStruct((m, n), BF16),
        compiler_params=params(),
        cost_estimate=cost(2 * rows * m * n, 2 * (rows * (m + n) + m * n)),
        name=name,
    )(a, b)


def input_kernel(
    x_ref, dq_ref, dk_ref, dv_ref, dr_ref, w_ref, gain_ref, out_ref, s_gain_ref, s_shift_ref, s_bq_ref, s_bv_ref
):
    width = x_ref.shape[1]
    xhat, inv_std = norm_forward(x_ref[...].astype(F32))
    da = mm_nt(dq_ref[...], w_ref[:, 0:width])
    da += mm_nt(dk_ref[...], w_ref[:, width : 2 * width])
    da += mm_nt(dv_ref[...], w_ref[:, 2 * width : 3 * width])
    first = pl.program_id(0) == 0

    def add_sum(ref, value):
        part = jnp.sum(value, axis=0, keepdims=True)
        ref[...] = jnp.where(first, part, ref[...] + part)

    add_sum(s_gain_ref, da * xhat)
    add_sum(s_shift_ref, da)
    add_sum(s_bq_ref, dq_ref[...].astype(F32))
    add_sum(s_bv_ref, dv_ref[...].astype(F32))
    out_ref[...] = dr_ref[...] + norm_backward(da, xhat, inv_std, gain_ref[...])


def input_grad(x, dq, dk, dv, dr, w_qkv, gain):
    rows, width = x.shape
    row = rows_spec(TILE, width)
    acc = pl.BlockSpec((1, width), lambda i: (0, 0))
    vec = jax.ShapeDtypeStruct((1, width), F32)
    return pl.pallas_call(
        input_kernel,
        grid=(rows // TILE,),
        in_specs=[row, row, row, row, row, whole(w_qkv.shape), whole((1, width))],
        out_specs=[row, acc, acc, acc, acc],
        out_shape=[jax.ShapeDtypeStruct((rows, width), F32), vec, vec, vec, vec],
        compiler_params=params(),
        cost_estimate=cost(6 * rows * width * width, 16 * rows * width),
        name="input_grad",
    )(x, dq, dk, dv, dr, w_qkv, gain)


def mask_terms(lengths, cells, context):
    usable = (jnp.arange(context) < lengths[0]) & (cells[0] == 1)
    bias = jnp.where(usable, 0.0, MASKED)
    kbias = jnp.broadcast_to(bias.astype(BF16)[:, None], (context, 128))
    rbias = bias[None, :]
    valid = jnp.broadcast_to(
        (jnp.arange(context) < lengths[0]).astype(F32)[:, None], (context, 128)
    )
    return kbias, rbias, valid


def gather(x):
    return lax.all_gather(x, "fsdp", axis=0, tiled=True)


def reduce_rows(x):
    rows = lax.psum_scatter(x, "fsdp", scatter_dimension=0, tiled=True)
    return lax.psum(rows, "dp").astype(F32)


def per_device(
    tokens, lengths, cells, cotangent, ln1_gain, ln1_bias, w_qkv, b_query, b_value, w_out, b_out,
    ln2_gain, ln2_bias, w_up, b_up, w_down, b_down,
):
    seqs, context, width = tokens.shape
    vectors = (ln1_gain, ln1_bias, b_query, b_value, b_out, ln2_gain, ln2_bias, b_down, b_up)
    sizes = [v.shape[0] for v in vectors]
    packed = lax.all_gather(jnp.concatenate(vectors), "fsdp", axis=0).astype(F32)
    edges = [sum(sizes[:i]) for i in range(len(sizes) + 1)]
    g1, h1, bq, bv, bo, g2, h2, bd, bu = (
        packed[:, a:b].reshape(1, -1) for a, b in zip(edges[:-1], edges[1:])
    )
    qkv_full = gather(w_qkv)
    out_full = gather(w_out)
    up_full = gather(w_up)
    down_full = gather(w_down)
    x = tokens[0]
    kbias, rbias, valid = mask_terms(lengths, cells, context)
    a1, qkv = qkv_forward(x, qkv_full, g1, h1, bq, bv, 0.125)
    o, qa = attn_forward(qkv, kbias, rbias)
    out, dm, a2, g, du, dr, dy, do, s_g2, s_h2, s_bu, s_bd, s_bo = mlp_both(
        x, o, cotangent[0], valid, out_full, up_full, down_full, bo, g2, h2, bu, bd
    )
    grad_down = reduce_rows(weight_grad(g, dm, "grad_down"))
    grad_up = reduce_rows(weight_grad(a2, du, "grad_up"))
    grad_out = reduce_rows(weight_grad(o, dy, "grad_out"))
    dq, dk, dv = attn_backward(qa, qkv, o, do, kbias, 0, width // 128)
    grad_qkv = reduce_rows(
        jnp.concatenate([weight_grad(a1, t, "grad_qkv") for t in (dq, dk, dv)], axis=1)
    )
    grad_x, s_g1, s_h1, s_bq, s_bv = input_grad(x, dq, dk, dv, dr, qkv_full, g1)
    shards = packed.shape[0]
    sums = jnp.concatenate(
        [s.reshape(shards, -1) for s in (s_g1, s_h1, s_bq, s_bv, s_bo, s_g2, s_h2, s_bd, s_bu)], axis=1
    )
    mine = lax.psum(sums, ("dp", "fsdp"))[lax.axis_index("fsdp")]
    g_g1, g_h1, g_bq, g_bv, g_bo, g_g2, g_h2, g_bd, g_bu = (
        mine[a:b] for a, b in zip(edges[:-1], edges[1:])
    )
    return (
        out[None], grad_x[None], g_g1, g_h1, grad_qkv, g_bq, g_bv, grad_out, g_bo, g_g2, g_h2,
        grad_up, g_bu, grad_down, g_bd,
    )


def solution(mesh):
    split = P(("dp", "fsdp"), None, None)
    vec, mat = P("fsdp"), P("fsdp", None)
    in_specs = (
        split, P(("dp", "fsdp")), P(("dp", "fsdp"), None), split,
        vec, vec, mat, vec, vec, mat, vec, vec, vec, mat, vec, mat, vec,
    )
    out_specs = (split, split, vec, vec, mat, vec, vec, mat, vec, vec, vec, mat, vec, mat, vec)
    return jax.shard_map(
        per_device, mesh=mesh, in_specs=in_specs, out_specs=out_specs, check_vma=False
    )
```

time: 652 us -> 502 us (0.77); the launches traced: 642 us -> 501 us
  matrix products: 307 us -> 0 us
  Pallas kernels: 0 us -> 147 us
  waiting for transfers between devices: 121 us -> 263 us
  local copies, waits for them, and re-layouts: 57.5 us -> 10.5 us
  other arithmetic: 54 us -> 12.1 us
  blocking collectives: 83.5 us -> 53.9 us
    dot_general x96 -> x0, matrix products: 307 us -> none  [the longest x12 45.3 us: head_backward(): jnp.einsum('sqd,skd->sqk', query_head, key_head, preferred_element_type=j...]
    pallas_call x0 -> x11, Pallas kernels: none -> 147 us  [the longest x6 38.4 us: weight_grad(): pl.pallas_call(partial(grad_kernel, tall), grid=(max(m, n) // tile,), in_...]
    all_gather x4, waiting for transfers between devices: 9.15 us -> 115 us  [gather(): return lax.all_gather(x, 'fsdp', axis=0, tiled=True)]
    reduce_scatter x4, waiting for transfers between devices: 57.6 us -> 134 us  [reduce_rows(): rows = lax.psum_scatter(x, 'fsdp', scatter_dimension=0, tiled=True)]
    unnamed x2 -> x0, blocking collectives: 60.8 us -> none
    psum x1, waiting for transfers between devices: 51.9 us -> 11.7 us  [reduce_rows(): return lax.psum(rows, 'dp').astype(F32)]
    psum x1, blocking collectives: 9.99 us -> 38 us  [per_device(): mine = lax.psum(sums, ('dp', 'fsdp'))[lax.axis_index('fsdp')]]
    unnamed x103 -> x44, local copies, waits for them, and re-layouts: 27.4 us -> 0.71 us
  transfers between devices with their start and end apart: 9 -> 9, of which waited for: 4 -> 7; matrix products, arithmetic and copies ran while one was open for 56% -> 3% of each run, Pallas kernels for 0% -> 21%
where the time goes in v1:
time: 502 us; the launch traced here: 501 us
  waiting for transfers between devices  263 us (52%)
  Pallas kernels  147 us (29%)
  blocking collectives  53.9 us (11%)
  between operations  14.8 us (3%)
  other arithmetic  12.1 us (2%)
  local copies, waits for them, and re-layouts  10.5 us (2%)
    reduce_scatter x4, waiting for transfers between devices, reduce_rows(): rows = lax.psum_scatter(x, 'fsdp', scatter_dimension=0, tiled=True)  134 us
    all_gather x4, waiting for transfers between devices, gather(): return lax.all_gather(x, 'fsdp', axis=0, tiled=True)  115 us
    pallas_call x6, Pallas kernels, weight_grad(): pl.pallas_call(partial(grad_kernel, tall), grid=(max(m, n) // tile,), in_...  38.4 us
    psum x1, blocking collectives, per_device(): mine = lax.psum(sums, ('dp', 'fsdp'))[lax.axis_index('fsdp')]  38 us
    pallas_call x1, Pallas kernels, mlp_both(): pl.pallas_call(mlp_kernel, grid=(rows // TILE,), in_specs=[row, row, row,...  35 us
    pallas_call x1, Pallas kernels, attn_backward(): pl.pallas_call(attn_bwd_kernel, grid=(pair_count,), in_specs=[pl.BlockSpe...  30.7 us
    pallas_call x1, Pallas kernels, attn_forward(): pl.pallas_call(attn_fwd_kernel, grid=(pairs,), in_specs=[part(0), part(1)...  23.7 us
    all_gather x1, blocking collectives, per_device(): lax.all_gather(jnp.concatenate(vectors), 'fsdp', axis=0).astype(F32)  15.9 us
  transfers between devices with their start and end apart: 9, of which 7 were waited for; matrix products, arithmetic and copies ran while one was open for 3% of the time, Pallas kernels for 21%

profile of v1, /device:TPU:0, one launch (start us, length us, event | category | flops | bytes accessed | tf_op | source)
XLA Modules:
  0.0 501.2 jit_solution(13553147399848398446)
XLA Ops:
  8.1 0.7 all-gather.9.cloned.1.call-update
  10.3 15.9 %all-gather.1 = bf16[8,1,1152]{2,1,0:T(2,128)(2,1)S(1)} all-gather(bf16[1,1,1152]{2,1,0:T(2,128)(2,1)S(1)} %reshape.137), channel_id=2, replica_groups=mesh['dp'=4,'fsdp'=8] {'fsdp'}, dimensions={0}, use_global_device_ids=true | all-gather | bytes 20736 | tf_op jit(solution)/shard_map/all_gather | solution.py:470
  33.5 20.5 %all-gather.7.cloned.1.call-done.w_ref = bf16[768,2304]{1,0:T(8,128)(2,1)} async-done(((bf16[96,2304]{1,0:T(8,128)(2,1)}), bf16[768,2304]{1,0:T(8,128)(2,1)}) %all-gather.7.cloned.1.call-update) | async-done | bytes 3538960 | tf_op jit(solution)/shard_map/all_gather | solution.py:455
  54.0 8.5 %qkv_forward.1 = (bf16[1024,768]{1,0:T(8,128)(2,1)}, bf16[1024,2304]{1,0:T(8,128)(2,1)}) custom-call(bf16[1024,768]{1,0:T(8,128)(2,1)} %bitcast.35, bf16[768,2304]{1,0:T(8,128)(2,1)} %all-gather.7.cloned.1.call-done.w_ref, f32[1,768]{1,0:T(1,128)} %reshape.117.gain_ref, f32[1,768]{1,0:T(1,128)} %reshape.118.shift_ref, f32[1,768]{1,0:T(1,128)} %reshape.119.bq_ref, ...), custom_call_target="tpu_custom_call" | custom-call | flops 3623878656 | bytes 9437184 | tf_op jit(solution)/shard_map/qkv_forward/pallas_call | solution.py:95
  62.5 0.9 broadcast_in_dim.33.kbias_ref
  63.4 23.7 %attn_forward.1 = (bf16[1024,768]{1,0:T(8,128)(2,1)}, bf16[1024,1536]{1,0:T(8,128)(2,1)}) custom-call(bf16[1024,2304]{1,0:T(8,128)(2,1)} %get-tuple-element.40.q_ref.k_ref.v_ref, bf16[1024,2304]{1,0:T(8,128)(2,1)} %get-tuple-element.40.q_ref.k_ref.v_ref, bf16[1024,2304]{1,0:T(8,128)(2,1)} %get-tuple-element.40.q_ref.k_ref.v_ref, ...), custom_call_target="tpu_custom_call" | custom-call | flops 6442450944 | bytes 9437184 | tf_op jit(solution)/shard_map/attn_forward/pallas_call | solution.py:173
  87.0 42.6 %all-gather.11.cloned.1.call-done.wu_ref = bf16[768,3072]{1,0:T(8,128)(2,1)} async-done(((bf16[96,3072]{1,0:T(8,128)(2,1)}), bf16[768,3072]{1,0:T(8,128)(2,1)}) %all-gather.11.cloned.1.call-update) | async-done | bytes 4718608 | tf_op jit(solution)/shard_map/all_gather | solution.py:455
  129.6 51.5 %all-gather.13.cloned.1.call-done.wd_ref = bf16[3072,768]{1,0:T(8,128)(2,1)} async-done(((bf16[384,768]{1,0:T(8,128)(2,1)}), bf16[3072,768]{1,0:T(8,128)(2,1)}) %all-gather.13.cloned.1.call-update) | async-done | bytes 4718608 | tf_op jit(solution)/shard_map/all_gather | solution.py:455
  181.1 1.0 broadcast_in_dim.36.valid_ref
  182.1 35.0 %mlp_both.1 = (bf16[1024,768]{1,0:T(8,128)(2,1)}, bf16[1024,768]{1,0:T(8,128)(2,1)}, bf16[1024,768]{1,0:T(8,128)(2,1)}, bf16[1024,3072]{1,0:T(8,128)(2,1)}, bf16...) custom-call(bf16[1024,768]{1,0:T(8,128)(2,1)} %bitcast.36, ...), custom_call_target="tpu_custom_call" | custom-call | flops 21743271936 | bytes 56623104 | tf_op jit(solution)/shard_map/mlp_both/pallas_call | solution.py:354
  217.1 4.6 grad_out.1
  221.7 30.7 %attn_backward.1 = (bf16[1024,768]{1,0:T(8,128)(2,1)}, bf16[1024,768]{1,0:T(8,128)(2,1)}, bf16[1024,768]{1,0:T(8,128)(2,1)}) custom-call(bf16[1024,1536]{1,0:T(8,128)(2,1)} %get-tuple-element.43.qa_ref, bf16[1024,2304]{1,0:T(8,128)(2,1)} %get-tuple-element.40.q_ref.k_ref.v_ref, bf16[1024,2304]{1,0:T(8,128)(2,1)} %get-tuple-element.40.q_ref.k_ref.v_ref, ...), custom_call_target="tpu_custom_call" | custom-call | flops 16106127360 | bytes 14155776 | tf_op jit(solution)/shard_map/attn_backward/pallas_call | solution.py:271
  252.5 4.5 grad_qkv.3
  257.0 4.5 grad_qkv.4
  261.5 4.6 grad_qkv.5
  266.2 2.9 pad_maximum_fusion
  269.1 10.1 %grad_down.1 = bf16[3072,768]{1,0:T(8,128)(2,1)} custom-call(bf16[1024,3072]{1,0:T(8,128)(2,1)} %get-tuple-element.63.a_ref, bf16[1024,768]{1,0:T(8,128)(2,1)} %get-tuple-element.64.refs_0_), custom_call_target="tpu_custom_call" | custom-call | flops 4831838208 | bytes 12582912 | tf_op jit(solution)/shard_map/grad_down/pallas_call | solution.py:393
  279.3 10.1 %grad_up.1 = bf16[768,3072]{1,0:T(8,128)(2,1)} custom-call(bf16[1024,768]{1,0:T(8,128)(2,1)} %get-tuple-element.61.a_ref, bf16[1024,3072]{1,0:T(8,128)(2,1)} %get-tuple-element.62.refs_0_), custom_call_target="tpu_custom_call" | custom-call | flops 4831838208 | bytes 12582912 | tf_op jit(solution)/shard_map/grad_up/pallas_call | solution.py:393
  289.5 22.2 %reduce-scatter.5.cloned.1.call-done = bf16[96,2304]{1,0:T(8,128)(2,1)} async-done(((bf16[768,2304]{1,0:T(8,128)(2,1)}), bf16[96,2304]{1,0:T(8,128)(2,1)}) %reduce-scatter.5.cloned.1.call-update) | async-done | bytes 442384 | tf_op jit(solution)/shard_map/reduce_scatter | solution.py:459
  311.7 55.7 %reduce-scatter.11.cloned.1.call-done = bf16[384,768]{1,0:T(8,128)(2,1)} async-done(((bf16[3072,768]{1,0:T(8,128)(2,1)}), bf16[384,768]{1,0:T(8,128)(2,1)}) %reduce-scatter.11.cloned.1.call-update) | async-done | bytes 589840 | tf_op jit(solution)/shard_map/reduce_scatter | solution.py:459
  367.5 55.7 %reduce-scatter.9.cloned.1.call-done = bf16[96,3072]{1,0:T(8,128)(2,1)} async-done(((bf16[768,3072]{1,0:T(8,128)(2,1)}), bf16[96,3072]{1,0:T(8,128)(2,1)}) %reduce-scatter.9.cloned.1.call-update) | async-done | bytes 589840 | tf_op jit(solution)/shard_map/reduce_scatter | solution.py:459
  423.2 10.7 %input_grad.1 = (f32[1024,768]{1,0:T(8,128)}, f32[1,768]{1,0:T(1,128)}, f32[1,768]{1,0:T(1,128)}, f32[1,768]{1,0:T(1,128)}, f32[1,768]{1,0:T(1,128)}) custom-call(bf16[1024,768]{1,0:T(8,128)(2,1)} %bitcast.37, bf16[1024,768]{1,0:T(8,128)(2,1)} %get-tuple-element.45.dq_ref.refs_0_, bf16[1024,768]{1,0:T(8,128)(2,1)} %get-tuple-element.46.dk_ref.refs_0_, ...), custom_call_target="tpu_custom_call" | custom-call | flops 3623878656 | bytes 12582912 | tf_op jit(solution)/shard_map/input_grad/pallas_call | solution.py:431
  433.9 0.7 reduce.1
  434.7 0.7 reduce.2
  435.4 0.7 reduce.3
  436.2 0.7 reduce.4
  438.7 38.0 %psum.35 = f32[8,1152]{1,0:T(8,128)S(1)} all-reduce(f32[8,1152]{1,0:T(8,128)S(1)} %concatenate.10), channel_id=1, replica_groups=mesh['dp'=4,'fsdp'=8] {'dp','fsdp'}, use_global_device_ids=true, to_apply=%region_0.1 | all-reduce | flops 9216 | bytes 73728 | tf_op jit(solution)/shard_map/psum | solution.py:498
  477.9 11.7 %all-reduce.3.cloned.1.call-done = (bf16[96,2304]{1,0:T(8,128)(2,1)}, bf16[96,768]{1,0:T(8,128)(2,1)}, bf16[96,3072]{1,0:T(8,128)(2,1)}, bf16[384,768]{1,0:T(8,128)(2,1)}) async-done(((bf16[96,2304]{1,0:T(8,128)(2,1)}, bf16[96,768]{1,0:T(8,128)(2,1)}, bf16[96,3072]{1,0:T(8,128)(2,1)}, bf16[384,768]{1,0:T(8,128)(2,1)}), (bf16[96,2304]{1,0:T(8,128)(2,1)}, bf16[96,768]{1,0:T(8,128)(2,1)}, ...) | async-done | bytes 1769488 | tf_op jit(solution)/shard_map/psum | solution.py:460
  489.6 2.3 convert_element_type.34
  491.9 1.1 convert_element_type.35
  493.0 1.0 convert_element_type.32
  494.0 0.7 convert_element_type.33
  (95 shorter events, 12.4 us)
Async XLA Ops:
  7.2 2.9 copy-start.12
  7.2 2.9 copy-start.13
  7.2 2.9 copy-start.14
  7.2 2.9 copy-start.15
  7.2 2.9 copy-start.16
  7.2 2.9 copy-start.17
  7.2 2.9 copy-start.18
  7.3 2.9 copy-start.11
  7.3 2.9 copy-start.19
  7.3 25.6 %copy-start.5 = (s32[1,1024]{1,0:T(1,128)S(1)}, s32[1,1024]{1,0:T(1,128)}, u32[]{:S(2)}) copy-start(s32[1,1024]{1,0:T(1,128)} %param.19) | copy-start | bytes 12292
  7.3 46.7 %all-gather.7.cloned.1.call-start = ((), (), s32[]{:S(2)}) async-start(), calls=%async_computation.4 | async-start | bytes 3981312 | tf_op jit(solution)/shard_map/all_gather | solution.py:455
  8.0 79.0 %all-gather.9.cloned.1.call-start = ((), (), s32[]{:S(2)}) async-start(), calls=%async_computation.5 | async-start | bytes 1327104 | tf_op jit(solution)/shard_map/all_gather | solution.py:455
  8.8 120.9 %all-gather.11.cloned.1.call-start = ((), (), s32[]{:S(2)}) async-start(), calls=%async_computation.6 | async-start | bytes 5308416 | tf_op jit(solution)/shard_map/all_gather | solution.py:455
  9.5 171.6 %all-gather.13.cloned.1.call-start = ((), (), s32[]{:S(2)}) async-start(), calls=%async_computation.7 | async-start | bytes 5308416 | tf_op jit(solution)/shard_map/all_gather | solution.py:455
  10.1 279.4 %reduce-scatter.7.cloned.1.call-start = ((), (), s32[]{:S(2)}) async-start(), calls=%async_computation.9 | async-start | bytes 1327104 | tf_op jit(solution)/shard_map/reduce_scatter | solution.py:459
  221.7 90.1 %reduce-scatter.5.cloned.1.call-start = ((), (), s32[]{:S(2)}) async-start(), calls=%async_computation.8 | async-start | bytes 3981312 | tf_op jit(solution)/shard_map/reduce_scatter | solution.py:459
  261.5 4.7 copy-start
  261.5 4.7 copy-start.1
  269.1 98.4 %reduce-scatter.11.cloned.1.call-start = ((), (), s32[]{:S(2)}) async-start(), calls=%async_computation.11 | async-start | bytes 5308416 | tf_op jit(solution)/shard_map/reduce_scatter | solution.py:459
  279.3 143.9 %reduce-scatter.9.cloned.1.call-start = ((), (), s32[]{:S(2)}) async-start(), calls=%async_computation.10 | async-start | bytes 5308416 | tf_op jit(solution)/shard_map/reduce_scatter | solution.py:459
  289.4 200.2 %all-reduce.3.cloned.1.call-start = ((), (), s32[]{:S(2)}) async-start(), calls=%async_computation.12 | async-start | bytes 3538944 | tf_op jit(solution)/shard_map/psum | solution.py:460
  423.2 14.3 %copy-start.6 = (f32[1,3072]{1,0:T(1,128)S(1)}, f32[1,3072]{1,0:T(1,128)}, u32[]{:S(2)}) copy-start(f32[1,3072]{1,0:T(1,128)} %get-tuple-element.58) | copy-start | bytes 36868
  423.2 15.0 %copy-start.10 = (f32[1,768]{1,0:T(1,128)S(1)}, f32[1,768]{1,0:T(1,128)}, u32[]{:S(2)}) copy-start(f32[1,768]{1,0:T(1,128)} %get-tuple-element.54) | copy-start | bytes 9220
  423.2 15.1 %copy-start.9 = (f32[1,768]{1,0:T(1,128)S(1)}, f32[1,768]{1,0:T(1,128)}, u32[]{:S(2)}) copy-start(f32[1,768]{1,0:T(1,128)} %get-tuple-element.55) | copy-start | bytes 9220
  423.2 15.2 %copy-start.8 = (f32[1,768]{1,0:T(1,128)S(1)}, f32[1,768]{1,0:T(1,128)}, u32[]{:S(2)}) copy-start(f32[1,768]{1,0:T(1,128)} %get-tuple-element.56) | copy-start | bytes 9220
  423.2 15.3 %copy-start.7 = (f32[1,768]{1,0:T(1,128)S(1)}, f32[1,768]{1,0:T(1,128)}, u32[]{:S(2)}) copy-start(f32[1,768]{1,0:T(1,128)} %get-tuple-element.57) | copy-start | bytes 9220
  489.6 2.3 copy-start.2
  489.6 3.4 copy-start.3
  491.9 2.1 copy-start.4
Sparse Core Ops, SparseCore 0:
  9.7 44.2 all-gather.6
  55.6 21.6 all-gather.8
  79.0 50.5 all-gather.10
  131.1 49.9 all-gather.12
  221.8 31.6 reduce-scatter.6
  269.2 42.4 reduce-scatter.4
  314.0 53.3 reduce-scatter.10
  369.8 53.3 reduce-scatter.8
  426.6 62.9 all-reduce.2
